TPU v7x, 256 devices: a whole 4x4x8 slice. The times are simulated.
256 devices in a mesh: row: 8 (over y, core), th: 8 (over z), ph: 4 (over x).
Axes of the slice: x: 4, y: 4, z: 8, core: 2. Of those that a mesh axis runs over, the one named last changes fastest.
Arguments:
- fields: float32 [6, 128, 128, 512], P(None, 'row', 'th', 'ph'), may hold values from -6 to 6
- lapse_field: float32 [128, 128, 512], P('row', 'th', 'ph'), may hold values from 0.3 to 1
- excision: int32 [128, 128, 512], P('row', 'th', 'ph'), may hold values 0 or 1
- sample_cells: int32 [128, 128, 4], P('row', 'th', 'ph'), may hold values from 0 to 127
- old_basis: float32 [252, 196608], P(None, ('row', 'th', 'ph'))
Outputs:
- new_fields: float32 [6, 128, 128, 512], P(None, 'row', 'th', 'ph')
- basis_out: float32 [256, 196608], P(None, ('row', 'th', 'ph'))
- factor: float32 [256, 256], replicated
Inputs may be any that keep to these rules, and one draw needn't show every extreme that they name: `excision`: 1 marks an excised cell.
All inputs are finite; a program needn't handle non-finite values. No bound on the sum of `excision` on one device may be relied on, other than what follows from the above.
Results may differ from a plain program's by a relative error of at most 0.007.
Values sent between devices are 32-bit elements; how exact they have to be, the bound alone decides.
A program may use at most 64 MiB of HBM per device.

v0:
```python
import math
import jax
import jax.numpy as jnp
from jax import lax
from jax.sharding import PartitionSpec as P

SPACING = 128
damping_rate = 3.0
time_step = 0.3
azimuth_gain = 5.0


def with_halo(block, sides, width, periodic):
    for axis, dim in sides:
        count = lax.axis_size(axis)
        forward = [(i, i + 1) for i in range(count - 1)]
        if periodic:
            forward.append((count - 1, 0))
        backward = [(target, source) for source, target in forward]
        low = lax.ppermute(
            lax.slice_in_dim(block, block.shape[dim] - width, None, axis=dim), axis, forward
        )
        high = lax.ppermute(lax.slice_in_dim(block, 0, width, axis=dim), axis, backward)
        block = jnp.concatenate([low, block, high], axis=dim)
    return block


def shifted(padded, axis_dim, offset):
    lengths = [padded.shape[0] - 4, padded.shape[1] - 4, padded.shape[2] - 4]
    starts = [2, 2, 2]
    starts[axis_dim] = 2 + offset
    return padded[
        starts[0] : starts[0] + lengths[0],
        starts[1] : starts[1] + lengths[1],
        starts[2] : starts[2] + lengths[2],
    ]


def derivative(padded, axis_dim):
    near_diff = shifted(padded, axis_dim, 1) - shifted(padded, axis_dim, -1)
    far_diff = shifted(padded, axis_dim, 2) - shifted(padded, axis_dim, -2)
    spacing_gain = azimuth_gain if axis_dim == 2 else 1.0
    return (8.0 * near_diff - far_diff) * (spacing_gain / 12.0)


def curl_of(padded, start_comp):
    first_part = padded[start_comp]
    second_part = padded[start_comp + 1]
    third_part = padded[start_comp + 2]
    return jnp.stack(
        [
            derivative(third_part, 1) - derivative(second_part, 2),
            derivative(first_part, 2) - derivative(third_part, 0),
            derivative(second_part, 0) - derivative(first_part, 1),
        ]
    )


def rates(padded, fields, damping):
    electric = curl_of(padded, 3) - damping_rate * damping * fields[:3]
    magnetic = -curl_of(padded, 0) - damping_rate * damping * fields[3:]
    return jnp.concatenate([electric, magnetic])


def padded_each(product):
    beside_all = with_halo(product, (("ph", 3),), 2, True)
    return with_halo(beside_all, (("row", 1), ("th", 2)), 2, False)


def on_device(fields, lapse_field, excision, sample_cells, old_basis):
    damping = excision.astype(jnp.float32)
    rad_cells = fields.shape[1]
    pol_cells = fields.shape[2]
    azi_cells = fields.shape[3]
    rad_total = rad_cells * lax.axis_size("row")
    pol_total = pol_cells * lax.axis_size("th")
    section_one = fields + time_step * rates(padded_each(lapse_field * fields), fields, damping)
    rate_two = rates(padded_each(lapse_field * section_one), section_one, damping)
    new_fields = 0.5 * (fields + section_one + time_step * rate_two)
    rad_index = (lax.axis_index("row") * rad_cells + jnp.arange(rad_cells)).astype(jnp.float32)
    pol_index = (lax.axis_index("th") * pol_cells + jnp.arange(pol_cells)).astype(jnp.float32)
    radius = 1.0 + 2.0 * (rad_index + 0.5) / rad_total
    polar = jnp.pi * (pol_index + 0.5) / pol_total
    weight = radius[:, None] * jnp.sqrt(jnp.sin(polar))[None, :]
    groups = azi_cells // SPACING
    chosen = jnp.arange(SPACING)[None, None, None, :] == sample_cells[:, :, :, None]
    weighted = jnp.where(chosen, weight[:, :, None, None], 0.0)

    def sample(field_set):
        grouped = field_set.reshape(6, rad_cells, pol_cells, groups, SPACING)
        return jnp.sum(grouped * weighted[None], axis=-1)

    snap_one = sample(section_one)
    snap_two = sample(new_fields)
    snapshot = jnp.stack(
        [
            snap_one[:3].reshape(-1),
            snap_one[3:].reshape(-1),
            snap_two[:3].reshape(-1),
            snap_two[3:].reshape(-1),
        ]
    )
    matrix = jnp.concatenate([old_basis, snapshot], axis=0)
    gram_sum = lax.psum(
        jnp.dot(matrix, matrix.T, precision=lax.Precision.HIGHEST), ("row", "th", "ph")
    )
    factor_low = lax.linalg.cholesky(gram_sum)
    solved = lax.linalg.triangular_solve(factor_low, matrix, left_side=True, lower=True)
    row_scale = math.sqrt(
        old_basis.shape[1] * lax.axis_size("row") * lax.axis_size("th") * lax.axis_size("ph")
    )
    return (new_fields, solved * row_scale, factor_low.T / row_scale)


def solution(mesh):
    return jax.shard_map(
        on_device,
        mesh=mesh,
        in_specs=(
            P(None, "row", "th", "ph"),
            P("row", "th", "ph"),
            P("row", "th", "ph"),
            P("row", "th", "ph"),
            P(None, ("row", "th", "ph")),
        ),
        out_specs=(P(None, "row", "th", "ph"), P(None, ("row", "th", "ph")), P()),
        check_vma=False,
    )
```

profile of v0, /device:TPU:2, one launch (start us, length us, event | category | flops | bytes accessed | tf_op | source)
XLA Modules:
  0.0 412.0 jit_solution(14045041573448911381)
XLA Ops:
  9.3 1.6 collective-permute-start
  12.3 1.9 collective-permute-done
  14.9 1.3 collective-permute-done.1
  17.0 1.3 collective-permute-start.2
  19.7 3.8 collective-permute-done.3
  24.2 3.8 collective-permute-start.4
  29.3 2.4 collective-permute-done.4
  31.7 4.4 %collective-permute-done.5 = f32[6,20,2,132]{3,2,1,0:T(2,128)S(1)} collective-permute-done((f32[6,20,2,132]{3,2,1,0:T(2,128)S(1)}, f32[6,20,2,132]{3,2,1,0:T(2,128)S(1)}, u32[]{:S(2)}, u32[]{:S(2)}) %collective-permute-start.5) | collective-permute-done | bytes 126752 | tf_op jit(solution)/shard_map/ppermute | solution.py:23
  44.3 1.9 collective-permute-done.6
  48.9 3.4 collective-permute-start.8
  53.6 6.2 %collective-permute-done.9 = f32[6,2,16,132]{3,2,1,0:T(8,128)S(1)} collective-permute-done((f32[6,2,16,132]{3,2,1,0:T(8,128)S(1)}, f32[6,2,16,132]{3,2,1,0:T(8,128)S(1)}, u32[]{:S(2)}, u32[]{:S(2)}) %collective-permute-start.9) | collective-permute-done | bytes 101408 | tf_op jit(solution)/shard_map/ppermute | solution.py:23
  60.6 3.8 collective-permute-start.10
  64.4 1.5 collective-permute-start.11
  66.0 2.1 collective-permute-done.10
  68.1 5.4 %collective-permute-done.11 = f32[6,20,2,132]{3,2,1,0:T(2,128)S(1)} collective-permute-done((f32[6,20,2,132]{3,2,1,0:T(2,128)S(1)}, f32[6,20,2,132]{3,2,1,0:T(2,128)S(1)}, u32[]{:S(2)}, u32[]{:S(2)}) %collective-permute-start.11) | collective-permute-done | bytes 126752 | tf_op jit(solution)/shard_map/ppermute | solution.py:23
  78.4 1.5 fusion.117
  80.0 259.2 %all-reduce.3.cloned.1.call-done = f32[256,256]{0,1:T(8,128)} async-done(((f32[256,256]{0,1:T(8,128)}), f32[256,256]{0,1:T(8,128)}) %all-reduce.3.cloned.1.call-update) | async-done | bytes 262160 | tf_op jit(solution)/shard_map/psum | solution.py:104
  341.3 11.7 %cholesky.50 = f32[128,128]{1,0:T(8,128)S(1)} custom-call(f32[128,128]{1,0:T(8,128)S(1)} %cholesky.118), custom_call_target="Cholesky" | custom-call | tf_op jit(solution)/shard_map/cholesky | solution.py:107
  353.1 9.8 %custom-call.11 = f32[1,128,128]{1,2,0:T(8,128)S(1)} custom-call(f32[1,128,128]{2,1,0:T(8,128)S(1)} %get-tuple-element.79), custom_call_target="InvertDiagBlocksLowerTriangular" | custom-call | tf_op jit(solution)/shard_map/cholesky | solution.py:107
  363.4 11.7 %cholesky.105 = f32[128,128]{1,0:T(8,128)S(1)} custom-call(f32[128,128]{1,0:T(8,128)S(1)} %convolution_subtract_fusion.1), custom_call_target="Cholesky" | custom-call | tf_op jit(solution)/shard_map/cholesky | solution.py:107
  377.9 4.0 while.1
  378.5 1.4 bitcast_dynamic-update-slice_fusion.2
  380.5 1.4 bitcast_dynamic-update-slice_fusion.2
  381.9 19.9 %custom-call.12 = f32[2,128,128]{1,2,0:T(8,128)S(1)} custom-call(f32[2,128,128]{2,1,0:T(8,128)S(1)} %get-tuple-element.10), custom_call_target="InvertDiagBlocksLowerTriangular" | custom-call | tf_op jit(solution)/shard_map/triangular_solve | solution.py:108
  (87 shorter events, 34.8 us)
Async XLA Ops:
  7.2 332.0 %all-reduce.3.cloned.1.call-start = ((), (), s32[]{:S(2)}) async-start(), calls=%async_computation | async-start | bytes 524288 | tf_op jit(solution)/shard_map/psum | solution.py:104
  9.3 4.9 %collective-permute-start = (f32[6,16,16,2]{2,1,3,0:T(8,128)S(1)}, f32[6,16,16,2]{2,1,3,0:T(8,128)S(1)}, u32[]{:S(2)}, u32[]{:S(2)}) collective-permute-start(f32[6,16,16,2]{2,1,3,0:T(8,128)S(1)} %copy.55), channel_id=1, source_target_pairs={{0,1},{1,2},{2,3},{3,0},{4,5},{5,6},{6,7},{7,4},{8,9},{9,10},{10,1... | collective-permute-start | bytes 36872 | tf_op jit(solution)/shard_map/ppermute | solution.py:20
  11.5 4.7 %collective-permute-start.1 = (f32[6,16,16,2]{2,1,3,0:T(8,128)S(1)}, f32[6,16,16,2]{2,1,3,0:T(8,128)S(1)}, u32[]{:S(2)}, u32[]{:S(2)}) collective-permute-start(f32[6,16,16,2]{2,1,3,0:T(8,128)S(1)} %copy.56), channel_id=1, source_target_pairs={{1,0},{2,1},{3,2},{0,3},{5,4},{6,5},{7,6},{4,7},{9,8},{10,9},{11,1... | collective-permute-start | bytes 36872 | tf_op jit(solution)/shard_map/ppermute | solution.py:23
  16.8 12.5 %copy-start.4 = (s32[16,16,128]{2,1,0:T(8,128)S(1)}, s32[16,16,128]{2,1,0:T(8,128)}, u32[]{:S(2)}) copy-start(s32[16,16,128]{2,1,0:T(8,128)} %param.7) | copy-start | bytes 393220
  17.0 2.6 collective-permute-start.2
  18.4 5.1 %collective-permute-start.3 = (f32[6,2,16,132]{3,2,1,0:T(8,128)S(1)}, f32[6,2,16,132]{3,2,1,0:T(8,128)S(1)}, u32[]{:S(2)}, u32[]{:S(2)}) collective-permute-start(f32[6,2,16,132]{3,2,1,0:T(8,128)S(1)} %get-tuple-element.57), channel_id=1, source_target_pairs={{32,0},{64,32},{96,64},{128,96},{160,128},{192,160},{224,192},{33,... | collective-permute-start | bytes 304136 | tf_op jit(solution)/shard_map/ppermute | solution.py:23
  24.2 7.5 %collective-permute-start.4 = (f32[6,20,2,132]{3,2,1,0:T(2,128)S(1)}, f32[6,20,2,132]{3,2,1,0:T(2,128)S(1)}, u32[]{:S(2)}, u32[]{:S(2)}) collective-permute-start(f32[6,20,2,132]{3,2,1,0:T(2,128)S(1)} %get-tuple-element.51), channel_id=1, source_target_pairs={{0,4},{4,8},{8,12},{12,16},{16,20},{20,24},{24,28},{1,5},{5,9},{9,... | collective-permute-start | bytes 380168 | tf_op jit(solution)/shard_map/ppermute | solution.py:20
  28.0 8.1 %collective-permute-start.5 = (f32[6,20,2,132]{3,2,1,0:T(2,128)S(1)}, f32[6,20,2,132]{3,2,1,0:T(2,128)S(1)}, u32[]{:S(2)}, u32[]{:S(2)}) collective-permute-start(f32[6,20,2,132]{3,2,1,0:T(2,128)S(1)} %get-tuple-element.52), channel_id=1, source_target_pairs={{4,0},{8,4},{12,8},{16,12},{20,16},{24,20},{28,24},{5,1},{9,5},{13... | collective-permute-start | bytes 380168 | tf_op jit(solution)/shard_map/ppermute | solution.py:23
  37.9 1.2 copy-start
  38.6 1.0 copy-start.3
  41.5 4.7 %collective-permute-start.6 = (f32[6,16,16,2]{2,1,3,0:T(8,128)S(1)}, f32[6,16,16,2]{2,1,3,0:T(8,128)S(1)}, u32[]{:S(2)}, u32[]{:S(2)}) collective-permute-start(f32[6,16,16,2]{2,1,3,0:T(8,128)S(1)} %copy.59), channel_id=1, source_target_pairs={{0,1},{1,2},{2,3},{3,0},{4,5},{5,6},{6,7},{7,4},{8,9},{9,10},{10,1... | collective-permute-start | bytes 36872 | tf_op jit(solution)/shard_map/ppermute | solution.py:20
  43.3 4.7 %collective-permute-start.7 = (f32[6,16,16,2]{2,1,3,0:T(8,128)S(1)}, f32[6,16,16,2]{2,1,3,0:T(8,128)S(1)}, u32[]{:S(2)}, u32[]{:S(2)}) collective-permute-start(f32[6,16,16,2]{2,1,3,0:T(8,128)S(1)} %copy.60), channel_id=1, source_target_pairs={{1,0},{2,1},{3,2},{0,3},{5,4},{6,5},{7,6},{4,7},{9,8},{10,9},{11,1... | collective-permute-start | bytes 36872 | tf_op jit(solution)/shard_map/ppermute | solution.py:23
  48.7 17.2 %copy-start.5 = (s32[16,16,1]{1,2,0:T(1,128)S(1)}, s32[16,16,1]{1,2,0:T(1,128)}, u32[]{:S(2)}) copy-start(s32[16,16,1]{1,2,0:T(1,128)} %param.8) | copy-start | bytes 3076
  48.9 4.8 %collective-permute-start.8 = (f32[6,2,16,132]{3,2,1,0:T(8,128)S(1)}, f32[6,2,16,132]{3,2,1,0:T(8,128)S(1)}, u32[]{:S(2)}, u32[]{:S(2)}) collective-permute-start(f32[6,2,16,132]{3,2,1,0:T(8,128)S(1)} %get-tuple-element.54), channel_id=1, source_target_pairs={{0,32},{32,64},{64,96},{96,128},{128,160},{160,192},{192,224},{1,3... | collective-permute-start | bytes 304136 | tf_op jit(solution)/shard_map/ppermute | solution.py:20
  52.3 7.6 %collective-permute-start.9 = (f32[6,2,16,132]{3,2,1,0:T(8,128)S(1)}, f32[6,2,16,132]{3,2,1,0:T(8,128)S(1)}, u32[]{:S(2)}, u32[]{:S(2)}) collective-permute-start(f32[6,2,16,132]{3,2,1,0:T(8,128)S(1)} %get-tuple-element.55), channel_id=1, source_target_pairs={{32,0},{64,32},{96,64},{128,96},{160,128},{192,160},{224,192},{33,... | collective-permute-start | bytes 304136 | tf_op jit(solution)/shard_map/ppermute | solution.py:23
  60.6 7.5 %collective-permute-start.10 = (f32[6,20,2,132]{3,2,1,0:T(2,128)S(1)}, f32[6,20,2,132]{3,2,1,0:T(2,128)S(1)}, u32[]{:S(2)}, u32[]{:S(2)}) collective-permute-start(f32[6,20,2,132]{3,2,1,0:T(2,128)S(1)} %get-tuple-element.49), channel_id=1, source_target_pairs={{0,4},{4,8},{8,12},{12,16},{16,20},{20,24},{24,28},{1,5},{5,9},{9,... | collective-permute-start | bytes 380168 | tf_op jit(solution)/shard_map/ppermute | solution.py:20
  64.4 9.1 %collective-permute-start.11 = (f32[6,20,2,132]{3,2,1,0:T(2,128)S(1)}, f32[6,20,2,132]{3,2,1,0:T(2,128)S(1)}, u32[]{:S(2)}, u32[]{:S(2)}) collective-permute-start(f32[6,20,2,132]{3,2,1,0:T(2,128)S(1)} %get-tuple-element.50), channel_id=1, source_target_pairs={{4,0},{8,4},{12,8},{16,12},{20,16},{24,20},{28,24},{5,1},{9,5},{13... | collective-permute-start | bytes 380168 | tf_op jit(solution)/shard_map/ppermute | solution.py:23
  75.1 1.5 copy-start.1
  76.6 1.6 copy-start.2
Sparse Core Ops, SparseCore 0:
  80.1 259.0 all-reduce.2
where the time goes:
time: 413 us; the launch traced here: 412 us
  waiting for transfers between devices  290 us (70%)
  other arithmetic  67.8 us (16%)
  starting transfers between devices  22.3 us (5%)
  between operations  15.7 us (4%)
  local copies, waits for them, and re-layouts  12.8 us (3%)
    psum x1, waiting for transfers between devices, on_device(): lax.psum(jnp.dot(matrix, matrix.T, precision=lax.Precision.HIGHEST), ('ro...  259 us
    another operation x7, other arithmetic, on_device(): factor_low = lax.linalg.cholesky(gram_sum)  34.6 us
    ppermute x6, waiting for transfers between devices, with_halo(): lax.ppermute(lax.slice_in_dim(block, 0, width, axis=dim), axis, backward)  22.4 us
    another operation x2, other arithmetic, on_device(): lax.linalg.triangular_solve(factor_low, matrix, left_side=True, lower=True)  19.9 us
    ppermute x6, starting transfers between devices, with_halo(): lax.ppermute(lax.slice_in_dim(block, block.shape[dim] - width, None, axis...  15.2 us
  transfers between devices with their start and end apart: 13, of which 11 were waited for; matrix products, arithmetic and copies ran while one was open for 1% of the time, Pallas kernels for 0%

commit v1 on v0

--- a/solution.py
+++ b/solution.py
@@ -102,7 +102,7 @@
     )
     matrix = jnp.concatenate([old_basis, snapshot], axis=0)
     gram_sum = lax.psum(
-        jnp.dot(matrix, matrix.T, precision=lax.Precision.HIGHEST), ("row", "th", "ph")
+        lax.psum(jnp.dot(matrix, matrix.T, precision=lax.Precision.HIGHEST), ("th", "ph")), "row"
     )
     factor_low = lax.linalg.cholesky(gram_sum)
     solved = lax.linalg.triangular_solve(factor_low, matrix, left_side=True, lower=True)

time: 413 us -> 368 us (0.89)
  waiting for transfers between devices: 290 us -> 246 us
    psum x1 -> x2, waiting for transfers between devices: 259 us -> 215 us  [the longest x1 149 us: on_device(): lax.psum(jnp.dot(matrix, matrix.T, precision=lax.Precision.HIGHEST), ('th...]
  transfers between devices with their start and end apart: 13 -> 14, of which waited for: 11 -> 12; matrix products, arithmetic and copies ran while one was open for 1% -> 1% of each run, Pallas kernels for 0% -> 0%
where the time goes in v1:
time: 368 us
  waiting for transfers between devices  246 us (67%)
  other arithmetic  67.6 us (18%)
  starting transfers between devices  22.3 us (6%)
  between operations  15.7 us (4%)
  local copies, waits for them, and re-layouts  12.8 us (3%)
    psum x1, waiting for transfers between devices, on_device(): lax.psum(jnp.dot(matrix, matrix.T, precision=lax.Precision.HIGHEST), ('th...  149 us
    psum x1, waiting for transfers between devices, on_device(): lax.psum(lax.psum(jnp.dot(matrix, matrix.T, precision=lax.Precision.HIGHE...  66 us
    another operation x7, other arithmetic, on_device(): factor_low = lax.linalg.cholesky(gram_sum)  34.6 us
    ppermute x6, waiting for transfers between devices, with_halo(): lax.ppermute(lax.slice_in_dim(block, 0, width, axis=dim), axis, backward)  22.4 us
    another operation x2, other arithmetic, on_device(): lax.linalg.triangular_solve(factor_low, matrix, left_side=True, lower=True)  19.7 us
    ppermute x6, starting transfers between devices, with_halo(): lax.ppermute(lax.slice_in_dim(block, block.shape[dim] - width, None, axis...  15.2 us
    ppermute x6, waiting for transfers between devices, with_halo(): lax.ppermute(lax.slice_in_dim(block, block.shape[dim] - width, None, axis...  8.16 us
  transfers between devices with their start and end apart: 14, of which 12 were waited for; matrix products, arithmetic and copies ran while one was open for 1% of the time, Pallas kernels for 0%

profile of v1, /device:TPU:2, one launch (start us, length us, event | category | flops | bytes accessed | tf_op | source)
XLA Modules:
  0.0 367.8 jit_solution(4200919090052524463)
XLA Ops:
  9.3 1.6 collective-permute-start
  12.3 1.9 collective-permute-done
  14.9 1.3 collective-permute-done.1
  19.7 3.8 %collective-permute-done.3 = f32[6,2,16,132]{3,2,1,0:T(8,128)S(1)} collective-permute-done((f32[6,2,16,132]{3,2,1,0:T(8,128)S(1)}, f32[6,2,16,132]{3,2,1,0:T(8,128)S(1)}, u32[]{:S(2)}, u32[]{:S(2)}) %collective-permute-start.3) | collective-permute-done | bytes 101408 | tf_op jit(solution)/shard_map/ppermute | solution.py:23
  24.2 3.8 %collective-permute-start.4 = (f32[6,20,2,132]{3,2,1,0:T(2,128)S(1)}, f32[6,20,2,132]{3,2,1,0:T(2,128)S(1)}, u32[]{:S(2)}, u32[]{:S(2)}) collective-permute-start(f32[6,20,2,132]{3,2,1,0:T(2,128)S(1)} %get-tuple-element.51), channel_id=1, source_target_pairs={{0,4},{4,8},{8,12},{12,16},{16,20},{20,24},{24,28},{1,5},{5,9},{9,... | collective-permute-start | bytes 380168 | tf_op jit(solution)/shard_map/ppermute | solution.py:20
  29.3 2.4 collective-permute-done.4
  31.7 4.4 %collective-permute-done.5 = f32[6,20,2,132]{3,2,1,0:T(2,128)S(1)} collective-permute-done((f32[6,20,2,132]{3,2,1,0:T(2,128)S(1)}, f32[6,20,2,132]{3,2,1,0:T(2,128)S(1)}, u32[]{:S(2)}, u32[]{:S(2)}) %collective-permute-start.5) | collective-permute-done | bytes 126752 | tf_op jit(solution)/shard_map/ppermute | solution.py:23
  44.3 1.9 collective-permute-done.6
  48.9 3.4 collective-permute-start.8
  53.6 6.2 %collective-permute-done.9 = f32[6,2,16,132]{3,2,1,0:T(8,128)S(1)} collective-permute-done((f32[6,2,16,132]{3,2,1,0:T(8,128)S(1)}, f32[6,2,16,132]{3,2,1,0:T(8,128)S(1)}, u32[]{:S(2)}, u32[]{:S(2)}) %collective-permute-start.9) | collective-permute-done | bytes 101408 | tf_op jit(solution)/shard_map/ppermute | solution.py:23
  60.6 3.8 %collective-permute-start.10 = (f32[6,20,2,132]{3,2,1,0:T(2,128)S(1)}, f32[6,20,2,132]{3,2,1,0:T(2,128)S(1)}, u32[]{:S(2)}, u32[]{:S(2)}) collective-permute-start(f32[6,20,2,132]{3,2,1,0:T(2,128)S(1)} %get-tuple-element.49), channel_id=1, source_target_pairs={{0,4},{4,8},{8,12},{12,16},{16,20},{20,24},{24,28},{1,5},{5,9},{9,... | collective-permute-start | bytes 380168 | tf_op jit(solution)/shard_map/ppermute | solution.py:20
  64.4 1.5 collective-permute-start.11
  66.0 2.1 collective-permute-done.10
  68.1 5.4 %collective-permute-done.11 = f32[6,20,2,132]{3,2,1,0:T(2,128)S(1)} collective-permute-done((f32[6,20,2,132]{3,2,1,0:T(2,128)S(1)}, f32[6,20,2,132]{3,2,1,0:T(2,128)S(1)}, u32[]{:S(2)}, u32[]{:S(2)}) %collective-permute-start.11) | collective-permute-done | bytes 126752 | tf_op jit(solution)/shard_map/ppermute | solution.py:23
  78.4 1.5 fusion.117
  80.0 149.0 %all-reduce.4.cloned.1.call-done = f32[256,256]{0,1:T(8,128)} async-done(((f32[256,256]{0,1:T(8,128)}), f32[256,256]{0,1:T(8,128)}) %all-reduce.4.cloned.1.call-update) | async-done | bytes 262160 | tf_op jit(solution)/shard_map/psum | solution.py:105
  229.1 66.0 %all-reduce.6.cloned.1.call-done = f32[256,256]{0,1:T(8,128)} async-done(((f32[256,256]{0,1:T(8,128)}), f32[256,256]{0,1:T(8,128)}) %all-reduce.6.cloned.1.call-update) | async-done | bytes 262160 | tf_op jit(solution)/shard_map/psum | solution.py:104
  297.2 11.7 %cholesky.50 = f32[128,128]{1,0:T(8,128)S(1)} custom-call(f32[128,128]{1,0:T(8,128)S(1)} %cholesky.118), custom_call_target="Cholesky" | custom-call | tf_op jit(solution)/shard_map/cholesky | solution.py:107
  308.9 9.8 %custom-call.11 = f32[1,128,128]{1,2,0:T(8,128)S(1)} custom-call(f32[1,128,128]{2,1,0:T(8,128)S(1)} %get-tuple-element.79), custom_call_target="InvertDiagBlocksLowerTriangular" | custom-call | tf_op jit(solution)/shard_map/cholesky | solution.py:107
  319.2 11.7 %cholesky.105 = f32[128,128]{1,0:T(8,128)S(1)} custom-call(f32[128,128]{1,0:T(8,128)S(1)} %convolution_subtract_fusion.1), custom_call_target="Cholesky" | custom-call | tf_op jit(solution)/shard_map/cholesky | solution.py:107
  333.8 4.2 %while.1 = (s32[]{:T(128)}, f32[256,256]{1,0:T(8,128)S(1)}, s32[2,2]{1,0:T(2,128)S(1)}, f32[2,128,128]{2,1,0:T(8,128)S(1)}, s32[]{:T(128)}) while((s32[]{:T(128)}, f32[256,256]{1,0:T(8,128)S(1)}, s32[2,2]{1,0:T(2,128)S(1)}, f32[2,128,128]{2,1,0:T(8,128)S(1)}, s32[]{:T(128)}) %tuple.61), condition=%wide.while_cond, body=%wide.while_body.sunk | while | flops 2 | bytes 131181 | solution.py:108
  334.5 1.4 bitcast_dynamic-update-slice_fusion.2
  336.6 1.4 bitcast_dynamic-update-slice_fusion.2
  338.0 19.7 %custom-call.12 = f32[2,128,128]{1,2,0:T(8,128)S(1)} custom-call(f32[2,128,128]{2,1,0:T(8,128)S(1)} %get-tuple-element.10), custom_call_target="InvertDiagBlocksLowerTriangular" | custom-call | tf_op jit(solution)/shard_map/triangular_solve | solution.py:108
  (90 shorter events, 36.2 us)
Async XLA Ops:
  7.2 221.9 %all-reduce.4.cloned.1.call-start = ((), (), s32[]{:S(2)}) async-start(), calls=%async_computation | async-start | bytes 524288 | tf_op jit(solution)/shard_map/psum | solution.py:105
  9.3 4.9 %collective-permute-start = (f32[6,16,16,2]{2,1,3,0:T(8,128)S(1)}, f32[6,16,16,2]{2,1,3,0:T(8,128)S(1)}, u32[]{:S(2)}, u32[]{:S(2)}) collective-permute-start(f32[6,16,16,2]{2,1,3,0:T(8,128)S(1)} %copy.55), channel_id=1, source_target_pairs={{0,1},{1,2},{2,3},{3,0},{4,5},{5,6},{6,7},{7,4},{8,9},{9,10},{10,1... | collective-permute-start | bytes 36872 | tf_op jit(solution)/shard_map/ppermute | solution.py:20
  11.5 4.7 %collective-permute-start.1 = (f32[6,16,16,2]{2,1,3,0:T(8,128)S(1)}, f32[6,16,16,2]{2,1,3,0:T(8,128)S(1)}, u32[]{:S(2)}, u32[]{:S(2)}) collective-permute-start(f32[6,16,16,2]{2,1,3,0:T(8,128)S(1)} %copy.56), channel_id=1, source_target_pairs={{1,0},{2,1},{3,2},{0,3},{5,4},{6,5},{7,6},{4,7},{9,8},{10,9},{11,1... | collective-permute-start | bytes 36872 | tf_op jit(solution)/shard_map/ppermute | solution.py:23
  16.8 12.5 %copy-start.4 = (s32[16,16,128]{2,1,0:T(8,128)S(1)}, s32[16,16,128]{2,1,0:T(8,128)}, u32[]{:S(2)}) copy-start(s32[16,16,128]{2,1,0:T(8,128)} %param.7) | copy-start | bytes 393220
  17.0 2.6 collective-permute-start.2
  18.4 5.1 %collective-permute-start.3 = (f32[6,2,16,132]{3,2,1,0:T(8,128)S(1)}, f32[6,2,16,132]{3,2,1,0:T(8,128)S(1)}, u32[]{:S(2)}, u32[]{:S(2)}) collective-permute-start(f32[6,2,16,132]{3,2,1,0:T(8,128)S(1)} %get-tuple-element.57), channel_id=1, source_target_pairs={{32,0},{64,32},{96,64},{128,96},{160,128},{192,160},{224,192},{33,... | collective-permute-start | bytes 304136 | tf_op jit(solution)/shard_map/ppermute | solution.py:23
  24.2 7.5 %collective-permute-start.4 = (f32[6,20,2,132]{3,2,1,0:T(2,128)S(1)}, f32[6,20,2,132]{3,2,1,0:T(2,128)S(1)}, u32[]{:S(2)}, u32[]{:S(2)}) collective-permute-start(f32[6,20,2,132]{3,2,1,0:T(2,128)S(1)} %get-tuple-element.51), channel_id=1, source_target_pairs={{0,4},{4,8},{8,12},{12,16},{16,20},{20,24},{24,28},{1,5},{5,9},{9,... | collective-permute-start | bytes 380168 | tf_op jit(solution)/shard_map/ppermute | solution.py:20
  28.0 8.1 %collective-permute-start.5 = (f32[6,20,2,132]{3,2,1,0:T(2,128)S(1)}, f32[6,20,2,132]{3,2,1,0:T(2,128)S(1)}, u32[]{:S(2)}, u32[]{:S(2)}) collective-permute-start(f32[6,20,2,132]{3,2,1,0:T(2,128)S(1)} %get-tuple-element.52), channel_id=1, source_target_pairs={{4,0},{8,4},{12,8},{16,12},{20,16},{24,20},{28,24},{5,1},{9,5},{13... | collective-permute-start | bytes 380168 | tf_op jit(solution)/shard_map/ppermute | solution.py:23
  37.9 1.2 copy-start
  38.6 1.0 copy-start.3
  41.5 4.7 %collective-permute-start.6 = (f32[6,16,16,2]{2,1,3,0:T(8,128)S(1)}, f32[6,16,16,2]{2,1,3,0:T(8,128)S(1)}, u32[]{:S(2)}, u32[]{:S(2)}) collective-permute-start(f32[6,16,16,2]{2,1,3,0:T(8,128)S(1)} %copy.59), channel_id=1, source_target_pairs={{0,1},{1,2},{2,3},{3,0},{4,5},{5,6},{6,7},{7,4},{8,9},{9,10},{10,1... | collective-permute-start | bytes 36872 | tf_op jit(solution)/shard_map/ppermute | solution.py:20
  43.3 4.7 %collective-permute-start.7 = (f32[6,16,16,2]{2,1,3,0:T(8,128)S(1)}, f32[6,16,16,2]{2,1,3,0:T(8,128)S(1)}, u32[]{:S(2)}, u32[]{:S(2)}) collective-permute-start(f32[6,16,16,2]{2,1,3,0:T(8,128)S(1)} %copy.60), channel_id=1, source_target_pairs={{1,0},{2,1},{3,2},{0,3},{5,4},{6,5},{7,6},{4,7},{9,8},{10,9},{11,1... | collective-permute-start | bytes 36872 | tf_op jit(solution)/shard_map/ppermute | solution.py:23
  48.7 17.2 %copy-start.5 = (s32[16,16,1]{1,2,0:T(1,128)S(1)}, s32[16,16,1]{1,2,0:T(1,128)}, u32[]{:S(2)}) copy-start(s32[16,16,1]{1,2,0:T(1,128)} %param.8) | copy-start | bytes 3076
  48.9 4.8 %collective-permute-start.8 = (f32[6,2,16,132]{3,2,1,0:T(8,128)S(1)}, f32[6,2,16,132]{3,2,1,0:T(8,128)S(1)}, u32[]{:S(2)}, u32[]{:S(2)}) collective-permute-start(f32[6,2,16,132]{3,2,1,0:T(8,128)S(1)} %get-tuple-element.54), channel_id=1, source_target_pairs={{0,32},{32,64},{64,96},{96,128},{128,160},{160,192},{192,224},{1,3... | collective-permute-start | bytes 304136 | tf_op jit(solution)/shard_map/ppermute | solution.py:20
  52.3 7.6 %collective-permute-start.9 = (f32[6,2,16,132]{3,2,1,0:T(8,128)S(1)}, f32[6,2,16,132]{3,2,1,0:T(8,128)S(1)}, u32[]{:S(2)}, u32[]{:S(2)}) collective-permute-start(f32[6,2,16,132]{3,2,1,0:T(8,128)S(1)} %get-tuple-element.55), channel_id=1, source_target_pairs={{32,0},{64,32},{96,64},{128,96},{160,128},{192,160},{224,192},{33,... | collective-permute-start | bytes 304136 | tf_op jit(solution)/shard_map/ppermute | solution.py:23
  60.6 7.5 %collective-permute-start.10 = (f32[6,20,2,132]{3,2,1,0:T(2,128)S(1)}, f32[6,20,2,132]{3,2,1,0:T(2,128)S(1)}, u32[]{:S(2)}, u32[]{:S(2)}) collective-permute-start(f32[6,20,2,132]{3,2,1,0:T(2,128)S(1)} %get-tuple-element.49), channel_id=1, source_target_pairs={{0,4},{4,8},{8,12},{12,16},{16,20},{20,24},{24,28},{1,5},{5,9},{9,... | collective-permute-start | bytes 380168 | tf_op jit(solution)/shard_map/ppermute | solution.py:20
  64.4 9.1 %collective-permute-start.11 = (f32[6,20,2,132]{3,2,1,0:T(2,128)S(1)}, f32[6,20,2,132]{3,2,1,0:T(2,128)S(1)}, u32[]{:S(2)}, u32[]{:S(2)}) collective-permute-start(f32[6,20,2,132]{3,2,1,0:T(2,128)S(1)} %get-tuple-element.50), channel_id=1, source_target_pairs={{4,0},{8,4},{12,8},{16,12},{20,16},{24,20},{28,24},{5,1},{9,5},{13... | collective-permute-start | bytes 380168 | tf_op jit(solution)/shard_map/ppermute | solution.py:23
  75.1 1.5 copy-start.1
  76.6 1.6 copy-start.2
  79.9 215.1 %all-reduce.6.cloned.1.call-start = ((), (), s32[]{:S(2)}) async-start(), calls=%async_computation.1 | async-start | bytes 524288 | tf_op jit(solution)/shard_map/psum | solution.py:104
Sparse Core Ops, SparseCore 0:
  80.1 148.9 all-reduce.3
  231.3 63.6 all-reduce.5
